TPU v7x, 256 devices: a whole 4x4x8 slice. The times are simulated.
256 devices in a mesh: clusters: 8 (over y, x_hi), members: 32 (over z, x_lo, core).
Axes of the slice: x: 4 (x_hi: 2, x_lo: 2; x = x_hi * 2 + x_lo), y: 4, z: 8, core: 2. Of those that a mesh axis runs over, the one named last changes fastest.
Arguments:
- embeddings: float32 [131072, 1024], P(('clusters', 'members')), parts along dimension 0, as said below
- member_order: int32 [131072], P(('clusters', 'members')), parts along dimension 0, may hold values from 0 to 16383, each once
- threshold: float32 [8], P('clusters'), parts along dimension 0, may hold values from 0.25 to 0.5
Outputs:
- best_similarity: float32 [131072], P(('clusters', 'members')), parts along dimension 0
- excess: float32 [131072], P(('clusters', 'members')), parts along dimension 0
There are 8 independent parts, one for each index of `clusters`. A program takes and returns all parts, laid end to end along the dimension named above; each array names one. Nothing has to cross between parts.
Inputs may be any that keep to these rules, and one draw needn't show every extreme that they name: member_order holds each of 0 to 16383 once. real-valued embeddings.
All inputs are finite; a program needn't handle non-finite values.
Results may differ from a plain program's by a relative error of at most 0.00051.
Values may be sent and summed in bfloat16 or wider, within the bound.
A program may use at most 128 MiB of HBM per device.

v0:
```python
import jax
import jax.numpy as jnp
from jax import lax
from jax.sharding import PartitionSpec as P


def block_scores(unit, other):
    return lax.dot_general(
        unit, other, (((1,), (1,)), ((), ())), preferred_element_type=jnp.float32
    )


def shards(embeddings, member_order, threshold):
    unit = (
        embeddings * lax.rsqrt(jnp.sum(embeddings * embeddings, axis=1, keepdims=True) + 1e-06)
    ).astype(jnp.bfloat16)
    floor_value = jnp.float32(-1.0)
    start_best = jnp.full((unit.shape[0],), -1.0, jnp.float32)
    scores = block_scores(unit, lax.all_gather(unit, "members", axis=0, tiled=True))
    mask = (
        lax.all_gather(member_order, "members", axis=0, tiled=True)[None, :] < member_order[:, None]
    )
    best = jnp.maximum(start_best, jnp.max(jnp.where(mask, scores, floor_value), axis=1))
    excess = jnp.maximum(best - threshold[0], jnp.float32(0.0))
    return (best, excess)


def solution(mesh):
    placed = (P(("clusters", "members"), None), P(("clusters", "members")), P("clusters"))
    return jax.shard_map(
        shards,
        mesh=mesh,
        in_specs=placed,
        out_specs=(P(("clusters", "members")), P(("clusters", "members"))),
        check_vma=False,
    )
```

profile of v0, /device:TPU:1, one launch (start us, length us, event | category | flops | bytes accessed | tf_op | source)
XLA Modules:
  0.0 231.1 jit_solution(13599985710889065328)
XLA Ops:
  7.2 0.0 all-gather.3.cloned.1.call-start
  7.2 1.8 multiply_reduce_fusion
  9.0 2.8 %multiply_convert_fusion = bf16[512,1024]{1,0:T(8,128)(2,1)} fusion(f32[512,1024]{1,0:T(8,128)} %param.3, f32[512]{0:T(512)S(1)} %add_rsqrt_fusion), kind=kLoop, calls=%fused_computation.1 | loop fusion | flops 1048576 | bytes 3147776 | tf_op jit(solution)/shard_map/convert_element_type | solution.py:16
  11.8 0.0 all-gather.3.cloned.1.call-update
  12.5 39.5 %all-gather = s32[32,1,512]{2,1,0:T(1,128)S(1)} all-gather(s32[1,1,512]{2,1,0:T(1,128)} %bitcast.7), channel_id=1, replica_groups=mesh['clusters'=8,'members'=32] {'members'}, dimensions={0}, use_global_device_ids=true | all-gather | bytes 67584 | tf_op jit(solution)/shard_map/all_gather | solution.py:21
  51.9 148.5 %all-gather.3.cloned.1.call-done = bf16[16384,1024]{1,0:T(8,128)(2,1)} async-done(((bf16[512,1024]{1,0:T(8,128)(2,1)}), bf16[16384,1024]{1,0:T(8,128)(2,1)}) %all-gather.3.cloned.1.call-update) | async-done | bytes 33554448 | tf_op jit(solution)/shard_map/all_gather | solution.py:19
  200.5 23.2 %select_reduce_fusion = f32[512]{0:T(512)S(1)} fusion(bf16[512,1024]{1,0:T(8,128)(2,1)} %multiply_convert_fusion, bf16[16384,1024]{1,0:T(8,128)(2,1)} %all-gather.3.cloned.1.call-done, s32[16384]{0:T(1024)S(1)} %bitcast.6, s32[512]{0:T(512)} %param.4), kind=kOutput, calls=%fused_computation | convolution fusion | flops 17205035008 | bytes 34672640 | tf_op jit(solution)/shard_map/dot_general | solution.py:8
  223.7 0.6 subtract_maximum_fusion
  (1 shorter events, 0.0 us)
Async XLA Ops:
  7.2 193.3 %all-gather.3.cloned.1.call-start = ((), (), s32[]{:S(2)}) async-start(), calls=%async_computation | async-start | bytes 34603008 | tf_op jit(solution)/shard_map/all_gather | solution.py:19
Sparse Core Ops, SparseCore 0:
  11.9 188.4 all-gather.2
where the time goes:
time: 231 us
  waiting for transfers between devices  149 us (65%)
  blocking collectives  39.5 us (17%)
  matrix products  23.2 us (10%)
  between operations  14.7 us (6%)
  other arithmetic  5.16 us (2%)
    all_gather x1, waiting for transfers between devices, shards(): lax.all_gather(unit, 'members', axis=0, tiled=True)  149 us
    all_gather x1, blocking collectives, shards(): lax.all_gather(member_order, 'members', axis=0, tiled=True)[None, :]  39.5 us
    dot_general x1, matrix products, block_scores(): lax.dot_general(unit, other, (((1,), (1,)), ((), ())), preferred_element_...  23.2 us
  transfers between devices with their start and end apart: 1, of which 1 were waited for; matrix products, arithmetic and copies ran while one was open for 0% of the time, Pallas kernels for 0%

commit v1 on v0

--- a/solution.py
+++ b/solution.py
@@ -18,7 +18,11 @@
     start_best = jnp.full((unit.shape[0],), -1.0, jnp.float32)
     scores = block_scores(unit, lax.all_gather(unit, "members", axis=0, tiled=True))
     mask = (
-        lax.all_gather(member_order, "members", axis=0, tiled=True)[None, :] < member_order[:, None]
+        jnp.concatenate(
+            lax.all_to_all(jnp.stack([member_order] * lax.axis_size("members")), "members", 0, 0),
+            axis=0,
+        )[None, :]
+        < member_order[:, None]
     )
     best = jnp.maximum(start_best, jnp.max(jnp.where(mask, scores, floor_value), axis=1))
     excess = jnp.maximum(best - threshold[0], jnp.float32(0.0))

time: 231 us -> 231 us (level)
  blocking collectives: 39.5 us -> 0 us
  waiting for transfers between devices: 149 us -> 176 us
  starting transfers between devices: 0.04 us -> 11.1 us
    all_gather x1 -> x0, blocking collectives: 39.5 us -> none  [shards(): lax.all_gather(member_order, 'members', axis=0, tiled=True)[None, :]]
    all_gather x1, waiting for transfers between devices: 149 us -> 168 us  [shards(): lax.all_gather(unit, 'members', axis=0, tiled=True)]
    all_to_all x0 -> x1, starting transfers between devices: none -> 11 us  [shards(): lax.all_to_all(jnp.stack([member_order] * lax.axis_size('members')), 'mem...]
    all_to_all x0 -> x1, waiting for transfers between devices: none -> 7.62 us  [shards(): lax.all_to_all(jnp.stack([member_order] * lax.axis_size('members')), 'mem...]
  transfers between devices with their start and end apart: 1 -> 2, of which waited for: 1 -> 2; matrix products, arithmetic and copies ran while one was open for 0% -> 1% of each run, Pallas kernels for 0% -> 0%
where the time goes in v1:
time: 231 us
  waiting for transfers between devices  176 us (76%)
  matrix products  23.2 us (10%)
  between operations  14.7 us (6%)
  starting transfers between devices  11.1 us (5%)
  other arithmetic  5.16 us (2%)
    all_gather x1, waiting for transfers between devices, shards(): lax.all_gather(unit, 'members', axis=0, tiled=True)  168 us
    dot_general x1, matrix products, block_scores(): lax.dot_general(unit, other, (((1,), (1,)), ((), ())), preferred_element_...  23.2 us
    all_to_all x1, starting transfers between devices, shards(): lax.all_to_all(jnp.stack([member_order] * lax.axis_size('members')), 'mem...  11 us
    all_to_all x1, waiting for transfers between devices, shards(): lax.all_to_all(jnp.stack([member_order] * lax.axis_size('members')), 'mem...  7.62 us
  transfers between devices with their start and end apart: 2, of which 2 were waited for; matrix products, arithmetic and copies ran while one was open for 1% of the time, Pallas kernels for 0%

profile of v1, /device:TPU:1, one launch (start us, length us, event | category | flops | bytes accessed | tf_op | source)
XLA Modules:
  0.0 231.1 jit_solution(8264312339589648375)
XLA Ops:
  7.2 0.0 all-gather.2.cloned.1.call-start
  7.2 1.8 multiply_reduce_fusion
  9.0 2.8 %multiply_convert_fusion = bf16[512,1024]{1,0:T(8,128)(2,1)} fusion(f32[512,1024]{1,0:T(8,128)} %param.3, f32[512]{0:T(512)S(1)} %add_rsqrt_fusion), kind=kLoop, calls=%fused_computation.1 | loop fusion | flops 1048576 | bytes 3147776 | tf_op jit(solution)/shard_map/convert_element_type | solution.py:16
  11.8 0.0 all-gather.2.cloned.1.call-update
  11.8 1.3 stack.2
  13.1 11.0 %all-to-all-start = ((s32[32,1,512]{2,1,0:T(1,128)}), s32[32,1,512]{2,1,0:T(1,128)S(1)}, u32[]{:S(2)}, u32[]{:S(2)}) async-start(s32[32,1,512]{2,1,0:T(1,128)} %stack.2), calls=%async_computation | async-start | bytes 131072 | tf_op jit(solution)/shard_map/all_to_all | solution.py:22
  24.8 7.6 %all-to-all-done = s32[32,1,512]{2,1,0:T(1,128)S(1)} async-done(((s32[32,1,512]{2,1,0:T(1,128)}), s32[32,1,512]{2,1,0:T(1,128)S(1)}, u32[]{:S(2)}, u32[]{:S(2)}) %all-to-all-start) | async-done | bytes 65568 | tf_op jit(solution)/shard_map/all_to_all | solution.py:22
  32.4 168.0 %all-gather.2.cloned.1.call-done = bf16[16384,1024]{1,0:T(8,128)(2,1)} async-done(((bf16[512,1024]{1,0:T(8,128)(2,1)}), bf16[16384,1024]{1,0:T(8,128)(2,1)}) %all-gather.2.cloned.1.call-update) | async-done | bytes 33554448 | tf_op jit(solution)/shard_map/all_gather | solution.py:19
  200.4 23.2 %select_reduce_fusion = f32[512]{0:T(512)S(1)} fusion(bf16[512,1024]{1,0:T(8,128)(2,1)} %multiply_convert_fusion, bf16[16384,1024]{1,0:T(8,128)(2,1)} %all-gather.2.cloned.1.call-done, s32[16384]{0:T(1024)S(1)} %bitcast.5, s32[512]{0:T(512)} %param.4), kind=kOutput, calls=%fused_computation | convolution fusion | flops 17205035008 | bytes 34672640 | tf_op jit(solution)/shard_map/dot_general | solution.py:8
  223.6 0.6 subtract_maximum_fusion
  (1 shorter events, 0.0 us)
Async XLA Ops:
  7.2 193.2 %all-gather.2.cloned.1.call-start = ((), (), s32[]{:S(2)}) async-start(), calls=%async_computation.1 | async-start | bytes 34603008 | tf_op jit(solution)/shard_map/all_gather | solution.py:19
  13.1 19.3 %all-to-all-start = ((s32[32,1,512]{2,1,0:T(1,128)}), s32[32,1,512]{2,1,0:T(1,128)S(1)}, u32[]{:S(2)}, u32[]{:S(2)}) async-start(s32[32,1,512]{2,1,0:T(1,128)} %stack.2), calls=%async_computation | async-start | bytes 131072 | tf_op jit(solution)/shard_map/all_to_all | solution.py:22
Sparse Core Ops, SparseCore 0:
  11.9 188.4 all-gather.1
